TPU v7x, 128 devices: a whole 4x4x4 slice. The times are simulated.
128 devices in a mesh: dp: 1, tp: 16 (over z, y), fsdp: 8 (over x, core).
Axes of the slice: x: 4, y: 4, z: 4, core: 2. Of those that a mesh axis runs over, the one named last changes fastest.
Arguments:
- hidden: bfloat16 [8, 1024, 6144], P(('dp', 'fsdp'))
- positions: int32 [1024], replicated
- norm_gain: float32 [6144], P('fsdp')
- w_query: bfloat16 [6144, 6144], P('fsdp', 'tp')
- w_key: bfloat16 [6144, 96], P('fsdp')
- w_value: bfloat16 [6144, 96], P('fsdp')
- w_gate: bfloat16 [6144, 24576], P('fsdp', 'tp')
- w_up: bfloat16 [6144, 24576], P('fsdp', 'tp')
- w_out: bfloat16 [6144, 6144], P('tp', 'fsdp')
- w_down: bfloat16 [24576, 6144], P('tp', 'fsdp')
Outputs:
- output: bfloat16 [8, 1024, 6144], P(('dp', 'fsdp'))
All inputs are finite; a program needn't handle non-finite values.
Results may differ from a plain program's by a relative error of at most 0.0118586.
Values are sent between devices in bfloat16 or wider.
A program may use at most 1 GiB of HBM per device.

v0:
```python
import functools

import jax
import jax.numpy as jnp
import numpy as np
from jax import lax
from jax.experimental import pallas as pl
from jax.experimental.pallas import tpu as pltpu
from jax.sharding import PartitionSpec as P

MESH = pl.DeviceIdType.MESH
NORM_EPS = 1e-6


def rope_tables(positions, head_dim):
    inv_freq = 10000.0 ** (-jnp.arange(0, head_dim, 2, dtype=jnp.float32) / head_dim)
    angles = positions.astype(jnp.float32)[:, None] * inv_freq[None, :]
    angles = jnp.concatenate([angles, angles], axis=-1)
    return jnp.cos(angles), jnp.sin(angles)


FF_TILE = 256


def first_kernel(
    rows_hbm, gain_hbm, wq_hbm, wk_hbm, wv_hbm, wg_hbm, wu_hbm, cos_ref, sin_ref, pick_ref, pick_rot_ref, place_ref,
    attn_hbm, z_hbm,
    act, gains, wq, wk, wv, wff, q_heads, k_rot, values, zbuf,
    send_sem, recv_sem, gain_send, gain_recv, load_sem, act_sem, out_sem,
):
    n = 8
    fs = lax.axis_index("fsdp")
    core = lax.rem(fs, 2)
    chip = lax.div(fs, 2)
    depth = wq_hbm.shape[0]
    half = depth // 2
    seq_len = rows_hbm.shape[0]
    n_chunks = wg_hbm.shape[1] // FF_TILE

    def device(by_chip, other):
        c = core if not other else 1 - core
        return lax.rem(chip + by_chip + 4, 4) * 2 + c

    right, left, sib = ({"fsdp": device(*p)} for p in ((1, 0), (-1, 0), (0, 1)))
    places = [(0, 0), (0, 1), (-1, 0), (-1, 1), (1, 0), (1, 1), (2, 0), (2, 1)]

    barrier = pltpu.get_barrier_semaphore()
    for by in range(1, n):
        pl.semaphore_signal(barrier, inc=1, device_id={"fsdp": lax.rem(fs + by, n)}, device_id_type=MESH)
    pl.semaphore_wait(barrier, n - 1)

    def qkv_streams():
        return [(0, wq_hbm, lambda at: wq.at[at, :]), (1, wk_hbm, lambda at: wk.at[at, :]), (2, wv_hbm, lambda at: wv.at[at, :])]

    def ff_streams(c):
        cols = pl.ds(pl.multiple_of(c * FF_TILE, FF_TILE), FF_TILE)
        return [
            (3 + 2 * c, wg_hbm.at[:, cols], lambda at: wff.at[c, at, pl.ds(0, FF_TILE)]),
            (4 + 2 * c, wu_hbm.at[:, cols], lambda at: wff.at[c, at, pl.ds(FF_TILE, FF_TILE)]),
        ]

    messages = [
        (2 * depth, depth, None, right), (4 * depth, depth, None, left),
        (6 * depth, half, 2 * depth, right), (6 * depth + half, half, 4 * depth + half, left),
        (depth, depth, None, sib), (3 * depth, depth, 2 * depth, sib), (5 * depth, depth, 4 * depth, sib),
        (7 * depth, half, 6 * depth, sib), (7 * depth + half, half, 6 * depth + half, sib),
    ]

    def message(stream, idx):
        row, own, gathered = stream
        dst, size, src, peer = messages[idx]
        return pltpu.make_async_remote_copy(
            src_ref=own if src is None else gathered(pl.ds(src, size)), dst_ref=gathered(pl.ds(dst, size)),
            send_sem=send_sem.at[row, idx], recv_sem=recv_sem.at[row, idx], device_id=peer, device_id_type=MESH)

    def own_load(stream):
        row, own, gathered = stream
        return pltpu.make_async_copy(own, gathered(pl.ds(0, depth)), load_sem.at[row])

    def send(streams, *idxs):
        for idx in idxs:
            for stream in streams:
                message(stream, idx).start()

    def receive(streams, *idxs):
        for idx in idxs:
            for stream in streams:
                message(stream, idx).wait_recv()

    def begin(streams):
        send(streams, 0, 1, 4)
        for stream in streams:
            own_load(stream).start()

    def pass_on(streams):
        receive(streams, 0, 1)
        send(streams, 2, 3, 5, 6)

    def complete(streams):
        receive(streams, 2, 3)
        send(streams, 7, 8)
        for stream in streams:
            own_load(stream).wait()
        receive(streams, 4, 5, 6, 7, 8)

    def gain_copy(slot):
        by_chip, other = places[slot]
        return pltpu.make_async_remote_copy(
            src_ref=gain_hbm, dst_ref=gains.at[slot], send_sem=gain_send.at[slot], recv_sem=gain_recv.at[slot],
            device_id={"fsdp": device(-by_chip, other)}, device_id_type=MESH)

    for slot in range(1, n):
        gain_copy(slot).start()
    begin(qkv_streams())
    begin(ff_streams(0))
    own_gain = pltpu.make_async_copy(gain_hbm, gains.at[0], gain_send.at[0])
    own_gain.start()
    blocks = []
    for slot, place in enumerate(places):
        cols = pl.ds(pl.multiple_of(device(*place) * depth, 128), depth)
        blocks.append(pltpu.make_async_copy(rows_hbm.at[:, cols], act.at[:, pl.ds(slot * depth, depth)], act_sem.at[slot]))
    for block in blocks:
        block.start()
    own_gain.wait()
    for slot in range(1, n):
        gain_copy(slot).wait()
    for block in blocks:
        block.wait()

    @pl.loop(0, seq_len // 16)
    def _(r):
        where = pl.ds(pl.multiple_of(r * 16, 16), 16)
        row_f32 = act[where, :].astype(jnp.float32)
        centered = row_f32 - jnp.mean(row_f32, axis=-1, keepdims=True)
        variance = jnp.mean(centered * centered, axis=-1, keepdims=True)
        scaled = centered * lax.rsqrt(variance + NORM_EPS)
        for slot in range(n):
            cols = slice(slot * depth, (slot + 1) * depth)
            act[where, cols] = (scaled[:, cols] * gains[slot]).astype(jnp.bfloat16)

    pass_on(qkv_streams())
    begin(ff_streams(1))
    pass_on(ff_streams(0))
    begin(ff_streams(2))
    complete(qkv_streams())

    n_heads, _, head_dim = pick_ref.shape
    q_block = 256

    @pl.loop(0, seq_len // q_block)
    def _(m):
        where = pl.ds(pl.multiple_of(m * q_block, q_block), q_block)
        cos_t, sin_t = cos_ref[where, :], sin_ref[where, :]
        dot = functools.partial(jnp.dot, preferred_element_type=jnp.float32)
        query_raw = dot(act[where, :], wq[...]).astype(jnp.bfloat16)
        for h in range(n_heads):
            rotated = dot(query_raw, pick_ref[h]) * cos_t + dot(query_raw, pick_rot_ref[h]) * sin_t
            q_heads[h, where, :] = rotated.astype(jnp.bfloat16)
        key_raw = dot(act[where, :], wk[...]).astype(jnp.bfloat16)
        key_turned = dot(key_raw, pick_rot_ref[0, 0:head_dim, :])
        k_rot[where, :] = (key_raw.astype(jnp.float32) * cos_t + key_turned * sin_t).astype(jnp.bfloat16)
        values[where, :] = dot(act[where, :], wv[...]).astype(jnp.bfloat16)

    for idx in range(9):
        message(qkv_streams()[0], idx).wait_send()
    pass_on(ff_streams(1))
    begin(ff_streams(3))

    score_scale = head_dim ** -0.5
    for blk in range(seq_len // q_block):
        lo, hi = blk * q_block, (blk + 1) * q_block
        causal_mask = lax.broadcasted_iota(jnp.int32, (q_block, hi), 1) <= lo + lax.broadcasted_iota(jnp.int32, (q_block, hi), 0)
        wq[lo:hi, :] = jnp.zeros((q_block, wq.shape[1]), jnp.bfloat16)

        @pl.loop(0, n_heads)
        def _(h):
            scores = lax.dot_general(q_heads[h, lo:hi, :], k_rot[0:hi, :], (((1,), (1,)), ((), ())), preferred_element_type=jnp.float32) * score_scale
            scores = jnp.where(causal_mask, scores, -1e30)
            weights = jnp.exp(scores - jnp.max(scores, axis=-1, keepdims=True))
            prob_rows = (weights / jnp.sum(weights, axis=-1, keepdims=True)).astype(jnp.bfloat16)
            out = jnp.dot(prob_rows, values[0:hi, :], preferred_element_type=jnp.float32).astype(jnp.bfloat16)
            placed = jnp.dot(out, place_ref[h], preferred_element_type=jnp.float32).astype(jnp.bfloat16)
            wq[lo:hi, :] = wq[lo:hi, :] + placed

    attn_out = pltpu.make_async_copy(wq.at[pl.ds(0, seq_len), :], attn_hbm, out_sem.at[n_chunks])
    attn_out.start()

    def z_out(c):
        cols = pl.ds(pl.multiple_of(c * FF_TILE, FF_TILE), FF_TILE)
        return pltpu.make_async_copy(zbuf.at[lax.rem(c, 2)], z_hbm.at[:, cols], out_sem.at[c])

    @pl.loop(0, n_chunks)
    def _(c):
        @pl.when(c + 2 < n_chunks)
        def _():
            pass_on(ff_streams(c + 2))

        @pl.when(c + 4 < n_chunks)
        def _():
            begin(ff_streams(c + 4))

        complete(ff_streams(c))

        @pl.when(c >= 2)
        def _():
            z_out(c - 2).wait()

        @pl.loop(0, seq_len // 256)
        def _(m):
            where = pl.ds(pl.multiple_of(m * 256, 256), 256)
            both = jnp.dot(act[where, :], wff[c], preferred_element_type=jnp.float32)
            gate = both[:, :FF_TILE].astype(jnp.bfloat16).astype(jnp.float32)
            up = both[:, FF_TILE:].astype(jnp.bfloat16).astype(jnp.float32)
            zbuf[lax.rem(c, 2), where, :] = (gate * jax.nn.sigmoid(gate) * up).astype(jnp.bfloat16)

        z_out(c).start()

    for c in (n_chunks - 2, n_chunks - 1):
        z_out(c).wait()
    attn_out.wait()
    for stream in qkv_streams()[1:]:
        for idx in range(9):
            message(stream, idx).wait_send()

    @pl.loop(0, n_chunks)
    def _(c):
        for stream in ff_streams(c):
            for idx in range(9):
                message(stream, idx).wait_send()


def first_products(rows, norm_gain, w_query, w_key, w_value, w_gate, w_up, cos_t, sin_t):
    seq_len, width = rows.shape
    q_width, head_dim, ff = w_query.shape[1], w_key.shape[1], w_gate.shape[1]
    n_heads = q_width // head_dim
    n_chunks = ff // FF_TILE
    bf16 = jnp.bfloat16
    feature = np.arange(head_dim)
    head = np.arange(n_heads)[:, None, None] * head_dim
    source = np.arange(q_width)[None, :, None]
    one_hot = np.where(source == head + feature, 1.0, 0.0)
    turned = np.where(feature < head_dim // 2, feature + head_dim // 2, feature - head_dim // 2)
    sign = np.where(feature < head_dim // 2, -1.0, 1.0)
    pick = jnp.asarray(one_hot, bf16)
    pick_rot = jnp.asarray(np.where(source == head + turned, sign, 0.0), bf16)
    place = jnp.asarray(one_hot.transpose(0, 2, 1), bf16)
    hbm = pl.BlockSpec(memory_space=pl.ANY)
    vmem = pl.BlockSpec(memory_space=pltpu.VMEM)
    return pl.pallas_call(
        first_kernel,
        in_specs=[hbm] * 7 + [vmem] * 5,
        out_specs=[hbm, hbm],
        out_shape=[jax.ShapeDtypeStruct((seq_len, q_width), bf16), jax.ShapeDtypeStruct((seq_len, ff), bf16)],
        scratch_shapes=[
            pltpu.VMEM((seq_len, width), bf16),
            pltpu.VMEM((8, 1, width // 8), jnp.float32),
            pltpu.VMEM((width, q_width), bf16),
            pltpu.VMEM((width, head_dim), bf16),
            pltpu.VMEM((width, head_dim), bf16),
            pltpu.VMEM((n_chunks, width, 2 * FF_TILE), bf16),
            pltpu.VMEM((n_heads, seq_len, head_dim), bf16),
            pltpu.VMEM((seq_len, head_dim), bf16),
            pltpu.VMEM((seq_len, head_dim), bf16),
            pltpu.VMEM((2, seq_len, FF_TILE), bf16),
            pltpu.SemaphoreType.DMA((3 + 2 * n_chunks, 9)),
            pltpu.SemaphoreType.DMA((3 + 2 * n_chunks, 9)),
            pltpu.SemaphoreType.DMA((8,)),
            pltpu.SemaphoreType.DMA((8,)),
            pltpu.SemaphoreType.DMA((3 + 2 * n_chunks,)),
            pltpu.SemaphoreType.DMA((8,)),
            pltpu.SemaphoreType.DMA((n_chunks + 1,)),
        ],
        compiler_params=pltpu.CompilerParams(collective_id=1, has_side_effects=True, vmem_limit_bytes=67043328),
    )(rows, norm_gain.reshape(1, -1), w_query, w_key, w_value, w_gate, w_up, cos_t, sin_t, pick, pick_rot, place)


ROWS_L1 = 128
ROWS_L2 = 32
N_GROUPS = 8
BUBBLE = 3
STAGES = 9
PART_SLOTS = 5


def reduce_kernel(n_acts, *refs):
    acts_hbm = refs[:n_acts]
    reduce_body(acts_hbm, *refs[n_acts:])


def reduce_body(
    acts_hbm, wo_hbm, wd_hbm, rows_hbm, out_hbm,
    act, weight, part, whole, recv1, recv2, recv3, recv4, resid,
    send_sem, recv_sem, xsend_sem, xrecv_sem, load_sem, resid_sem, out_sem,
):
    n_fsdp = 8
    tp = lax.axis_index("tp")
    fs = lax.axis_index("fsdp")
    coord = {"y": lax.rem(tp, 4), "z": lax.div(tp, 4)}
    core = lax.rem(fs, 2)
    full = wo_hbm.shape[1]
    cols = full // 2
    split = wo_hbm.shape[0]

    def at(axis, delta):
        moved = lax.rem(coord[axis] + delta + 4, 4)
        return {"tp": coord["z"] * 4 + moved if axis == "y" else moved * 4 + coord["y"]}

    right = {"fsdp": lax.rem(fs + 2, n_fsdp)}
    left = {"fsdp": lax.rem(fs + n_fsdp - 2, n_fsdp)}
    sib = {"fsdp": fs + 1 - 2 * core}

    barrier = pltpu.get_barrier_semaphore()
    peers = [at("y", 1), at("y", -1), at("z", 1), at("z", -1), right, left, sib]
    for peer in peers:
        pl.semaphore_signal(barrier, inc=1, device_id=peer, device_id_type=MESH)
    pl.semaphore_wait(barrier, len(peers))

    def xcopy(src, slot, peer):
        return pltpu.make_async_remote_copy(
            src_ref=src, dst_ref=weight.at[slot], send_sem=xsend_sem.at[slot, 0], recv_sem=xrecv_sem.at[slot, 0],
            device_id=peer, device_id_type=MESH)

    def own_parts(half):
        where = pl.ds(half * cols, cols)
        return [(wo_hbm.at[:, where], pl.ds(0, split)), (wd_hbm.at[:, where], pl.ds(split, wd_hbm.shape[0]))]

    def own_copies(slot, peer):
        return [
            pltpu.make_async_remote_copy(
                src_ref=src, dst_ref=weight.at[slot, at], send_sem=xsend_sem.at[slot, j], recv_sem=xrecv_sem.at[slot, j],
                device_id=peer, device_id_type=MESH)
            for j, (src, at) in enumerate(own_parts(slot % 2))
        ]

    own_sends = [(4, right), (8, left), (2, sib), (5, right), (9, left), (3, sib)]
    relays = [(6, sib), (7, sib), (10, sib), (11, sib), (12, right), (13, left), (14, sib), (15, sib)]

    def x_wait_recv(slot):
        if slot in (2, 3, 4, 5, 8, 9):
            for copy in own_copies(slot, sib):
                copy.wait_recv()
        else:
            xcopy(weight.at[slot], slot, sib).wait_recv()

    for slot, peer in own_sends:
        for copy in own_copies(slot, peer):
            copy.start()
    loads = []
    for half in range(2):
        for j, (src, part_rows) in enumerate(own_parts(half)):
            loads.append(pltpu.make_async_copy(src, weight.at[half, part_rows], load_sem.at[2 * half + j]))
    col = 0
    for idx, act_hbm in enumerate(acts_hbm):
        size = act_hbm.shape[1]
        loads.append(pltpu.make_async_copy(act_hbm, act.at[:, pl.ds(col, size)], load_sem.at[4 + idx]))
        col += size
    for load in loads:
        load.start()
    for load in loads:
        load.wait()

    halves = [("y", "z"), ("z", "y")]

    def pslot(g):
        return lax.rem(g, PART_SLOTS)

    def block1(x, delta):
        k = lax.rem(coord[halves[x][0]] + delta + 4, 4)
        return pl.multiple_of(x * 4 * ROWS_L1 + k * ROWS_L1, ROWS_L1)

    def block2(x, delta):
        k = lax.rem(coord[halves[x][1]] + delta + 4, 4)
        return pl.multiple_of(block1(x, 0) + k * ROWS_L2, ROWS_L2)

    def offset(base, add):
        return pl.multiple_of(base + add, 16)

    def message(g, x, kind, src, dst, axis, delta):
        return pltpu.make_async_remote_copy(
            src_ref=src, dst_ref=dst, send_sem=send_sem.at[g, x, kind], recv_sem=recv_sem.at[g, x, kind],
            device_id=at(axis, delta), device_id_type=MESH)

    def scatter_far(g, x, level):
        block, axis, buf, rows, kind = (block1, halves[x][0], recv1, ROWS_L1, 0) if level == 1 else (block2, halves[x][1], recv3, ROWS_L2, 4)
        half = rows // 2
        far = block(x, 2)
        return [
            message(g, x, kind, part.at[pslot(g), pl.ds(far, half), :], buf.at[g, x, 0], axis, 1),
            message(g, x, kind + 1, part.at[pslot(g), pl.ds(offset(far, half), half), :], buf.at[g, x, 1], axis, -1),
        ]

    def scatter_near(g, x, level):
        block, axis, buf, rows, kind = (block1, halves[x][0], recv2, ROWS_L1, 2) if level == 1 else (block2, halves[x][1], recv4, ROWS_L2, 6)
        return [
            message(g, x, kind, part.at[pslot(g), pl.ds(block(x, 1), rows), :], buf.at[g, x, 0], axis, 1),
            message(g, x, kind + 1, part.at[pslot(g), pl.ds(block(x, -1), rows), :], buf.at[g, x, 1], axis, -1),
        ]

    def gather_near(g, x, level):
        block, axis, rows, kind = (block1, halves[x][0], ROWS_L1, 12) if level == 1 else (block2, halves[x][1], ROWS_L2, 8)
        mine = whole.at[g, pl.ds(block(x, 0), rows), :]
        return [message(g, x, kind, mine, mine, axis, 1), message(g, x, kind + 1, mine, mine, axis, -1)]

    def gather_far(g, x, level):
        block, axis, rows, kind = (block1, halves[x][0], ROWS_L1, 14) if level == 1 else (block2, halves[x][1], ROWS_L2, 10)
        half = rows // 2
        lo = whole.at[g, pl.ds(block(x, -1), half), :]
        hi = whole.at[g, pl.ds(offset(block(x, 1), half), half), :]
        return [message(g, x, kind, lo, lo, axis, 1), message(g, x, kind + 1, hi, hi, axis, -1)]

    def start(copies):
        for copy in copies:
            copy.start()

    def finish(copies):
        for copy in copies:
            copy.wait()

    def summed(g, row, rows, *refs):
        total = part[pslot(g), pl.ds(row, rows), :].astype(jnp.float32)
        for ref in refs:
            total = total + ref.astype(jnp.float32)
        return total.astype(jnp.bfloat16)

    def add_into(g, row, rows, *refs):
        part[pslot(g), pl.ds(row, rows), :] = summed(g, row, rows, *refs)

    def group_info(g):
        mid = jnp.logical_and(g >= 2, g < 6)
        i = g - 2
        odd = lax.rem(i + 2, 2)
        slot = jnp.where(g < 2, g, jnp.where(mid, 4 + 4 * odd + lax.div(i + 2, 2) - 1, g + 6))
        delta = jnp.where(g < 2, 0, jnp.where(mid, 2 * odd - 1, 2))
        half = jnp.where(mid, lax.div(i + 2, 2) - 1, lax.rem(g, 2))
        chip = lax.rem(lax.div(fs, 2) + delta + 4, 4)
        col_a = pl.multiple_of((chip * 2 + core) * full + half * cols, 128)
        col_b = pl.multiple_of((chip * 2 + 1 - core) * full + half * cols, 128)
        return slot, col_a, col_b

    def resid_copies(g):
        _, col_a, col_b = group_info(g)
        copies = []
        for x in range(2):
            for j, col in enumerate((col_a, col_b)):
                copies.append(pltpu.make_async_copy(
                    rows_hbm.at[pl.ds(block2(x, 0), ROWS_L2), pl.ds(col, cols)],
                    resid.at[g, x, :, pl.ds(j * cols, cols)], resid_sem.at[g, 2 * x + j]))
        return copies

    def out_copies(g):
        _, col_a, col_b = group_info(g)
        return [
            pltpu.make_async_copy(whole.at[g, :, pl.ds(j * cols, cols)], out_hbm.at[:, pl.ds(col, cols)], out_sem.at[g, j])
            for j, col in enumerate((col_a, col_b))
        ]

    def stage0(g):
        slot, _, _ = group_info(g)
        start(resid_copies(g))

        @pl.when(g == 2)
        def _():
            x_wait_recv(4)
            xcopy(weight.at[4], 6, sib).start()
            xcopy(weight.at[4], 12, right).start()
            x_wait_recv(8)
            xcopy(weight.at[8], 10, sib).start()

        @pl.when(g == 4)
        def _():
            x_wait_recv(5)
            xcopy(weight.at[5], 7, sib).start()
            x_wait_recv(9)
            xcopy(weight.at[9], 11, sib).start()
            xcopy(weight.at[9], 13, left).start()

        @pl.when(g == 6)
        def _():
            x_wait_recv(12)
            xcopy(weight.at[12], 14, sib).start()
            x_wait_recv(13)
            xcopy(weight.at[13], 15, sib).start()

        for known, known_slot in enumerate((2, 3, 6, 10, 7, 11, 14, 15)):
            @pl.when(g == known)
            def _():
                x_wait_recv(known_slot)

        @pl.loop(0, act.shape[0] // 256)
        def _(m):
            where = pl.ds(pl.multiple_of(m * 256, 256), 256)
            for j in range(2):
                value = jnp.dot(act[where, :], weight[slot + 2 * j], preferred_element_type=jnp.float32)
                part[pslot(g), where, j * cols : (j + 1) * cols] = value.astype(jnp.bfloat16)

        for x in range(2):
            start(scatter_far(g, x, 1))

    def scatter_mid(level):
        def run(g):
            buf = recv1 if level == 1 else recv3
            rows = ROWS_L1 if level == 1 else ROWS_L2
            block = block1 if level == 1 else block2
            for x in range(2):
                finish(scatter_far(g, x, level))
                add_into(g, block(x, 1), rows // 2, buf[g, x, 0])
                add_into(g, offset(block(x, -1), rows // 2), rows // 2, buf[g, x, 1])
            for x in range(2):
                start(scatter_near(g, x, level))
        return run

    def stage2(g):
        for x in range(2):
            finish(scatter_near(g, x, 1))
            add_into(g, block1(x, 0), ROWS_L1, recv2[g, x, 0], recv2[g, x, 1])
        for x in range(2):
            start(scatter_far(g, x, 2))

    def stage4(g):
        finish(resid_copies(g))
        for x in range(2):
            finish(scatter_near(g, x, 2))
            whole[g, pl.ds(block2(x, 0), ROWS_L2), :] = summed(g, block2(x, 0), ROWS_L2, recv4[g, x, 0], recv4[g, x, 1], resid[g, x])
        for x in range(2):
            start(gather_near(g, x, 2))

    def relay(done, then):
        def run(g):
            for x in range(2):
                finish(done[0](g, x, done[1]))
                start(then[0](g, x, then[1]))
        return run

    def stage8(g):
        for x in range(2):
            finish(gather_far(g, x, 1))
        start(out_copies(g))

    stages = [
        stage0, scatter_mid(1), stage2, scatter_mid(2), stage4,
        relay((gather_near, 2), (gather_far, 2)), relay((gather_far, 2), (gather_near, 1)),
        relay((gather_near, 1), (gather_far, 1)), stage8,
    ]

    @pl.loop(0, N_GROUPS + BUBBLE + STAGES - 1)
    def _(t):
        for s in reversed(range(STAGES)):
            d = t - s
            early = jnp.logical_and(d >= 0, d < 2)
            late = jnp.logical_and(d >= 2 + BUBBLE, d < N_GROUPS + BUBBLE)
            g = jnp.where(d < 2, d, d - BUBBLE)

            @pl.when(jnp.logical_or(early, late))
            def _():
                stages[s](g)

    @pl.loop(0, N_GROUPS)
    def _(g):
        finish(out_copies(g))

    for slot, peer in own_sends:
        for copy in own_copies(slot, peer):
            copy.wait_send()
    for slot, peer in relays:
        xcopy(weight.at[slot], slot, peer).wait_send()


def second_product(acts, w_out, w_down, rows):
    seq_len = rows.shape[0]
    depth = w_out.shape[0] + w_down.shape[0]
    wide = w_out.shape[1]
    cols = wide // 2
    bf16 = jnp.bfloat16
    return pl.pallas_call(
        functools.partial(reduce_kernel, len(acts)),
        in_specs=[pl.BlockSpec(memory_space=pl.ANY)] * (len(acts) + 3),
        out_specs=pl.BlockSpec(memory_space=pl.ANY),
        out_shape=jax.ShapeDtypeStruct(rows.shape, bf16),
        scratch_shapes=[
            pltpu.VMEM((seq_len, depth), bf16),
            pltpu.VMEM((16, depth, cols), bf16),
            pltpu.VMEM((PART_SLOTS, seq_len, wide), bf16),
            pltpu.VMEM((N_GROUPS, seq_len, wide), bf16),
            pltpu.VMEM((N_GROUPS, 2, 2, ROWS_L1 // 2, wide), bf16),
            pltpu.VMEM((N_GROUPS, 2, 2, ROWS_L1, wide), bf16),
            pltpu.VMEM((N_GROUPS, 2, 2, ROWS_L2 // 2, wide), bf16),
            pltpu.VMEM((N_GROUPS, 2, 2, ROWS_L2, wide), bf16),
            pltpu.VMEM((N_GROUPS, 2, ROWS_L2, wide), bf16),
            pltpu.SemaphoreType.DMA((N_GROUPS, 2, 16)),
            pltpu.SemaphoreType.DMA((N_GROUPS, 2, 16)),
            pltpu.SemaphoreType.DMA((16, 2)),
            pltpu.SemaphoreType.DMA((16, 2)),
            pltpu.SemaphoreType.DMA((4 + len(acts),)),
            pltpu.SemaphoreType.DMA((N_GROUPS, 4)),
            pltpu.SemaphoreType.DMA((N_GROUPS, 2)),
        ],
        compiler_params=pltpu.CompilerParams(collective_id=0, has_side_effects=True, vmem_limit_bytes=62 * 1024 * 1024),
        cost_estimate=pl.CostEstimate(
            flops=2 * seq_len * depth * rows.shape[1], bytes_accessed=2 * (seq_len * depth + 8 * depth * wide + 2 * rows.size), transcendentals=0),
    )(*acts, w_out, w_down, rows)


def solution(mesh):
    row_spec = P(("dp", "fsdp"), None, None)

    def local_layer(hidden, positions, norm_gain, w_query, w_key, w_value, w_gate, w_up, w_out, w_down):
        rows = hidden[0]
        cos_t, sin_t = rope_tables(positions, w_key.shape[1])
        acts = first_products(rows, norm_gain, w_query, w_key, w_value, w_gate, w_up, cos_t, sin_t)
        return second_product(acts, w_out, w_down, rows)[None]

    in_specs = (row_spec, P(None), P("fsdp"), P("fsdp", "tp"), P("fsdp", None), P("fsdp", None), P("fsdp", "tp"), P("fsdp", "tp"), P("tp", "fsdp"), P("tp", "fsdp"))
    return jax.shard_map(local_layer, mesh=mesh, in_specs=in_specs, out_specs=row_spec, check_vma=False)
```

profile of v0, /device:TPU:0, one launch (start us, length us, event | category | flops | bytes accessed | tf_op | source)
XLA Modules:
  0.0 415.1 jit_solution(11053745133628719877)
XLA Ops:
  0.0 1.3 reshape.11.gain_hbm
  1.3 0.7 convert_element_type.3
  2.0 1.7 copy.14.wk_hbm
  3.7 1.7 copy.15.wv_hbm
  5.4 0.2 broadcast_multiply_fusion
  5.6 2.9 fusion
  8.5 206.8 %shard_map.127 = (bf16[1024,384]{1,0:T(8,128)(2,1)}, bf16[1024,1536]{1,0:T(8,128)(2,1)}) custom-call(bf16[1024,6144]{1,0:T(8,128)(2,1)} %bitcast.3, f32[1,768]{1,0:T(1,128)} %reshape.11.gain_hbm, bf16[768,384]{1,0:T(8,128)(2,1)} %wq_hbm.1, bf16[768,96]{1,0:T(8,128)(2,1)} %copy.14.wk_hbm, bf16[768,96]{1,0:T(8,128)(2,1)} %copy.15.wv_hbm, ...), custom_call_target="tpu_custom_call" | custom-call | tf_op jit(solution)/shard_map/pallas_call | solution.py:249
  215.3 189.1 %shard_map.128 = bf16[1024,6144]{1,0:T(8,128)(2,1)} custom-call(bf16[1024,384]{1,0:T(8,128)(2,1)} %get-tuple-element.7.refs_0_, bf16[1024,1536]{1,0:T(8,128)(2,1)} %get-tuple-element.8.refs_1_, bf16[384,768]{1,0:T(8,128)(2,1)} %refs_2_.1, bf16[1536,768]{1,0:T(8,128)(2,1)} %refs_3_.1, bf16[1024,6144]{1,0:T(8,128)(2,1)} %bitcast.4), custom_call_target="tpu_custom_call" | custom-call | flops 24159191040 | bytes 52690944 | tf_op jit(solution)/shard_map/pallas_call | solution.py:574
  404.3 10.7 %copy.17 = bf16[1,1024,6144]{2,1,0:T(8,128)(2,1)} copy(bf16[1,1024,6144]{2,1,0:T(8,128)(2,1)} %bitcast.2) | data formatting | bytes 25165824
  (1 shorter events, 0.0 us)
where the time goes:
time: 415 us
  Pallas kernels  396 us (95%)
  local copies, waits for them, and re-layouts  15.4 us (4%)
    pallas_call x1, Pallas kernels, first_products(): pl.pallas_call(first_kernel, in_specs=[hbm] * 7 + [vmem] * 5, out_specs=[...  207 us
    pallas_call x1, Pallas kernels, second_product(): pl.pallas_call(functools.partial(reduce_kernel, len(acts)), in_specs=[pl....  189 us
    unnamed x3, local copies, waits for them, and re-layouts  14.2 us

commit v1 on v0

--- a/solution.py
+++ b/solution.py
@@ -50,7 +50,7 @@
     pl.semaphore_wait(barrier, n - 1)
 
     def qkv_streams():
-        return [(0, wq_hbm, lambda at: wq.at[at, :]), (1, wk_hbm, lambda at: wk.at[at, :]), (2, wv_hbm, lambda at: wv.at[at, :])]
+        return [(0, wq_hbm, lambda at: wq.at[at, :]), (1, wk_hbm, lambda at: wk.at[:, at]), (2, wv_hbm, lambda at: wv.at[:, at])]
 
     def ff_streams(c):
         cols = pl.ds(pl.multiple_of(c * FF_TILE, FF_TILE), FF_TILE)
@@ -145,6 +145,10 @@
     complete(qkv_streams())
 
     n_heads, _, head_dim = pick_ref.shape
+
+    def dot_t(a, b):
+        return lax.dot_general(a, b, (((1,), (1,)), ((), ())), preferred_element_type=jnp.float32)
+
     q_block = 256
 
     @pl.loop(0, seq_len // q_block)
@@ -156,10 +160,10 @@
         for h in range(n_heads):
             rotated = dot(query_raw, pick_ref[h]) * cos_t + dot(query_raw, pick_rot_ref[h]) * sin_t
             q_heads[h, where, :] = rotated.astype(jnp.bfloat16)
-        key_raw = dot(act[where, :], wk[...]).astype(jnp.bfloat16)
+        key_raw = dot_t(act[where, :], wk[...]).astype(jnp.bfloat16)
         key_turned = dot(key_raw, pick_rot_ref[0, 0:head_dim, :])
         k_rot[where, :] = (key_raw.astype(jnp.float32) * cos_t + key_turned * sin_t).astype(jnp.bfloat16)
-        values[where, :] = dot(act[where, :], wv[...]).astype(jnp.bfloat16)
+        values[where, :] = dot_t(act[where, :], wv[...]).astype(jnp.bfloat16)
 
     for idx in range(9):
         message(qkv_streams()[0], idx).wait_send()
@@ -174,7 +178,7 @@
 
         @pl.loop(0, n_heads)
         def _(h):
-            scores = lax.dot_general(q_heads[h, lo:hi, :], k_rot[0:hi, :], (((1,), (1,)), ((), ())), preferred_element_type=jnp.float32) * score_scale
+            scores = dot_t(q_heads[h, lo:hi, :], k_rot[0:hi, :]) * score_scale
             scores = jnp.where(causal_mask, scores, -1e30)
             weights = jnp.exp(scores - jnp.max(scores, axis=-1, keepdims=True))
             prob_rows = (weights / jnp.sum(weights, axis=-1, keepdims=True)).astype(jnp.bfloat16)
@@ -255,8 +259,8 @@
             pltpu.VMEM((seq_len, width), bf16),
             pltpu.VMEM((8, 1, width // 8), jnp.float32),
             pltpu.VMEM((width, q_width), bf16),
-            pltpu.VMEM((width, head_dim), bf16),
-            pltpu.VMEM((width, head_dim), bf16),
+            pltpu.VMEM((head_dim, width), bf16),
+            pltpu.VMEM((head_dim, width), bf16),
             pltpu.VMEM((n_chunks, width, 2 * FF_TILE), bf16),
             pltpu.VMEM((n_heads, seq_len, head_dim), bf16),
             pltpu.VMEM((seq_len, head_dim), bf16),
@@ -271,13 +275,13 @@
             pltpu.SemaphoreType.DMA((n_chunks + 1,)),
         ],
         compiler_params=pltpu.CompilerParams(collective_id=1, has_side_effects=True, vmem_limit_bytes=67043328),
-    )(rows, norm_gain.reshape(1, -1), w_query, w_key, w_value, w_gate, w_up, cos_t, sin_t, pick, pick_rot, place)
+    )(rows, norm_gain.reshape(1, -1), w_query, w_key.T, w_value.T, w_gate, w_up, cos_t, sin_t, pick, pick_rot, place)
 
 
 ROWS_L1 = 128
 ROWS_L2 = 32
 N_GROUPS = 8
-BUBBLE = 3
+PERIOD = 5
 STAGES = 9
 PART_SLOTS = 5
 
@@ -309,12 +313,6 @@
     left = {"fsdp": lax.rem(fs + n_fsdp - 2, n_fsdp)}
     sib = {"fsdp": fs + 1 - 2 * core}
 
-    barrier = pltpu.get_barrier_semaphore()
-    peers = [at("y", 1), at("y", -1), at("z", 1), at("z", -1), right, left, sib]
-    for peer in peers:
-        pl.semaphore_signal(barrier, inc=1, device_id=peer, device_id_type=MESH)
-    pl.semaphore_wait(barrier, len(peers))
-
     def xcopy(src, slot, peer):
         return pltpu.make_async_remote_copy(
             src_ref=src, dst_ref=weight.at[slot], send_sem=xsend_sem.at[slot, 0], recv_sem=xrecv_sem.at[slot, 0],
@@ -342,9 +340,6 @@
         else:
             xcopy(weight.at[slot], slot, sib).wait_recv()
 
-    for slot, peer in own_sends:
-        for copy in own_copies(slot, peer):
-            copy.start()
     loads = []
     for half in range(2):
         for j, (src, part_rows) in enumerate(own_parts(half)):
@@ -356,6 +351,16 @@
         col += size
     for load in loads:
         load.start()
+
+    barrier = pltpu.get_barrier_semaphore()
+    peers = [at("y", 1), at("y", -1), at("z", 1), at("z", -1), right, left, sib]
+    for peer in peers:
+        pl.semaphore_signal(barrier, inc=1, device_id=peer, device_id_type=MESH)
+    pl.semaphore_wait(barrier, len(peers))
+
+    for slot, peer in own_sends:
+        for copy in own_copies(slot, peer):
+            copy.start()
     for load in loads:
         load.wait()
 
@@ -542,15 +547,15 @@
         relay((gather_near, 1), (gather_far, 1)), stage8,
     ]
 
-    @pl.loop(0, N_GROUPS + BUBBLE + STAGES - 1)
+    @pl.loop(0, (N_GROUPS // 2 - 1) * PERIOD + 1 + STAGES)
     def _(t):
         for s in reversed(range(STAGES)):
             d = t - s
-            early = jnp.logical_and(d >= 0, d < 2)
-            late = jnp.logical_and(d >= 2 + BUBBLE, d < N_GROUPS + BUBBLE)
-            g = jnp.where(d < 2, d, d - BUBBLE)
-
-            @pl.when(jnp.logical_or(early, late))
+            pair, second = lax.div(d + 2 * PERIOD, PERIOD) - 2, lax.rem(d + 2 * PERIOD, PERIOD)
+            g = 2 * pair + second
+            inside = jnp.logical_and(d >= 0, d < (N_GROUPS // 2) * PERIOD)
+
+            @pl.when(jnp.logical_and(inside, second < 2))
             def _():
                 stages[s](g)
 

time: 415 us -> 416 us (level)
    pallas_call x1, Pallas kernels: 189 us -> 197 us  [second_product(): pl.pallas_call(functools.partial(reduce_kernel, len(acts)), in_specs=[pl....]
    unnamed x3 -> x1, local copies, waits for them, and re-layouts: 14.2 us -> 10.7 us
where the time goes in v1:
time: 416 us
  Pallas kernels  400 us (96%)
  local copies, waits for them, and re-layouts  12 us (3%)
    pallas_call x1, Pallas kernels, first_products(): pl.pallas_call(first_kernel, in_specs=[hbm] * 7 + [vmem] * 5, out_specs=[...  204 us
    pallas_call x1, Pallas kernels, second_product(): pl.pallas_call(functools.partial(reduce_kernel, len(acts)), in_specs=[pl....  197 us
    unnamed x1, local copies, waits for them, and re-layouts  10.7 us

profile of v1, /device:TPU:0, one launch (start us, length us, event | category | flops | bytes accessed | tf_op | source)
XLA Modules:
  0.0 416.0 jit_solution(9708370014059939943)
XLA Ops:
  0.0 1.3 reshape.11.gain_hbm
  1.3 0.7 convert_element_type.3
  2.0 0.2 broadcast_multiply_fusion
  2.2 2.9 fusion
  5.1 203.6 %shard_map.127 = (bf16[1024,384]{1,0:T(8,128)(2,1)}, bf16[1024,1536]{1,0:T(8,128)(2,1)}) custom-call(bf16[1024,6144]{1,0:T(8,128)(2,1)} %bitcast.5, f32[1,768]{1,0:T(1,128)} %reshape.11.gain_hbm, bf16[768,384]{1,0:T(8,128)(2,1)} %wq_hbm.1, bf16[96,768]{1,0:T(8,128)(2,1)} %bitcast.7, bf16[96,768]{1,0:T(8,128)(2,1)} %bitcast.8, bf16[768,1536]{1,0:T(8,128)(2,1)} %wg_hbm.1, ...), custom_call_target="tpu_custom_call" | custom-call | tf_op jit(solution)/shard_map/pallas_call | solution.py:253
  208.7 196.6 %shard_map.128 = bf16[1024,6144]{1,0:T(8,128)(2,1)} custom-call(bf16[1024,384]{1,0:T(8,128)(2,1)} %get-tuple-element.7.refs_0_, bf16[1024,1536]{1,0:T(8,128)(2,1)} %get-tuple-element.8.refs_1_, bf16[384,768]{1,0:T(8,128)(2,1)} %refs_2_.1, bf16[1536,768]{1,0:T(8,128)(2,1)} %refs_3_.1, bf16[1024,6144]{1,0:T(8,128)(2,1)} %bitcast.6), custom_call_target="tpu_custom_call" | custom-call | flops 24159191040 | bytes 52690944 | tf_op jit(solution)/shard_map/pallas_call | solution.py:579
  405.3 10.7 %copy.15 = bf16[1,1024,6144]{2,1,0:T(8,128)(2,1)} copy(bf16[1,1024,6144]{2,1,0:T(8,128)(2,1)} %bitcast.4) | data formatting | bytes 25165824
  (1 shorter events, 0.0 us)

commit v2 on v1

--- a/solution.py
+++ b/solution.py
@@ -23,10 +23,10 @@
 
 
 def first_kernel(
-    rows_hbm, gain_hbm, wq_hbm, wk_hbm, wv_hbm, wg_hbm, wu_hbm, cos_ref, sin_ref, pick_ref, pick_rot_ref, place_ref,
-    attn_hbm, z_hbm,
+    rows_hbm, gain_hbm, wq_hbm, wk_hbm, wv_hbm, wg_hbm, wu_hbm, wo_hbm, cos_ref, sin_ref, pick_ref, pick_rot_ref, place_ref,
+    attn_hbm, z_hbm, pre_hbm,
     act, gains, wq, wk, wv, wff, q_heads, k_rot, values, zbuf,
-    send_sem, recv_sem, gain_send, gain_recv, load_sem, act_sem, out_sem,
+    send_sem, recv_sem, gain_send, gain_recv, load_sem, act_sem, out_sem, pre_send, pre_recv,
 ):
     n = 8
     fs = lax.axis_index("fsdp")
@@ -189,6 +189,11 @@
     attn_out = pltpu.make_async_copy(wq.at[pl.ds(0, seq_len), :], attn_hbm, out_sem.at[n_chunks])
     attn_out.start()
 
+    def w_out_copy(side):
+        return pltpu.make_async_remote_copy(
+            src_ref=wo_hbm, dst_ref=pre_hbm.at[side], send_sem=pre_send.at[side], recv_sem=pre_recv.at[side],
+            device_id=(right, left)[side], device_id_type=MESH)
+
     def z_out(c):
         cols = pl.ds(pl.multiple_of(c * FF_TILE, FF_TILE), FF_TILE)
         return pltpu.make_async_copy(zbuf.at[lax.rem(c, 2)], z_hbm.at[:, cols], out_sem.at[c])
@@ -198,6 +203,11 @@
         @pl.when(c + 2 < n_chunks)
         def _():
             pass_on(ff_streams(c + 2))
+
+        @pl.when(c + 2 == n_chunks - 1)
+        def _():
+            for side in range(2):
+                w_out_copy(side).start()
 
         @pl.when(c + 4 < n_chunks)
         def _():
@@ -222,6 +232,8 @@
     for c in (n_chunks - 2, n_chunks - 1):
         z_out(c).wait()
     attn_out.wait()
+    for side in range(2):
+        w_out_copy(side).wait()
     for stream in qkv_streams()[1:]:
         for idx in range(9):
             message(stream, idx).wait_send()
@@ -233,7 +245,7 @@
                 message(stream, idx).wait_send()
 
 
-def first_products(rows, norm_gain, w_query, w_key, w_value, w_gate, w_up, cos_t, sin_t):
+def first_products(rows, norm_gain, w_query, w_key, w_value, w_gate, w_up, w_out, cos_t, sin_t):
     seq_len, width = rows.shape
     q_width, head_dim, ff = w_query.shape[1], w_key.shape[1], w_gate.shape[1]
     n_heads = q_width // head_dim
@@ -252,9 +264,9 @@
     vmem = pl.BlockSpec(memory_space=pltpu.VMEM)
     return pl.pallas_call(
         first_kernel,
-        in_specs=[hbm] * 7 + [vmem] * 5,
-        out_specs=[hbm, hbm],
-        out_shape=[jax.ShapeDtypeStruct((seq_len, q_width), bf16), jax.ShapeDtypeStruct((seq_len, ff), bf16)],
+        in_specs=[hbm] * 8 + [vmem] * 5,
+        out_specs=[hbm] * 3,
+        out_shape=[jax.ShapeDtypeStruct((seq_len, q_width), bf16), jax.ShapeDtypeStruct((seq_len, ff), bf16), jax.ShapeDtypeStruct((2, *w_out.shape), bf16)],
         scratch_shapes=[
             pltpu.VMEM((seq_len, width), bf16),
             pltpu.VMEM((8, 1, width // 8), jnp.float32),
@@ -273,17 +285,19 @@
             pltpu.SemaphoreType.DMA((3 + 2 * n_chunks,)),
             pltpu.SemaphoreType.DMA((8,)),
             pltpu.SemaphoreType.DMA((n_chunks + 1,)),
+            pltpu.SemaphoreType.DMA((2,)),
+            pltpu.SemaphoreType.DMA((2,)),
         ],
         compiler_params=pltpu.CompilerParams(collective_id=1, has_side_effects=True, vmem_limit_bytes=67043328),
-    )(rows, norm_gain.reshape(1, -1), w_query, w_key.T, w_value.T, w_gate, w_up, cos_t, sin_t, pick, pick_rot, place)
+    )(rows, norm_gain.reshape(1, -1), w_query, w_key.T, w_value.T, w_gate, w_up, w_out, cos_t, sin_t, pick, pick_rot, place)
 
 
 ROWS_L1 = 128
 ROWS_L2 = 32
 N_GROUPS = 8
-PERIOD = 5
+PERIOD = 3
 STAGES = 9
-PART_SLOTS = 5
+PART_SLOTS = 6
 
 
 def reduce_kernel(n_acts, *refs):
@@ -292,7 +306,7 @@
 
 
 def reduce_body(
-    acts_hbm, wo_hbm, wd_hbm, rows_hbm, out_hbm,
+    acts_hbm, pre_hbm, wo_hbm, wd_hbm, rows_hbm, out_hbm,
     act, weight, part, whole, recv1, recv2, recv3, recv4, resid,
     send_sem, recv_sem, xsend_sem, xrecv_sem, load_sem, resid_sem, out_sem,
 ):
@@ -313,9 +327,12 @@
     left = {"fsdp": lax.rem(fs + n_fsdp - 2, n_fsdp)}
     sib = {"fsdp": fs + 1 - 2 * core}
 
+    def slot_ref(slot, rows=slice(None)):
+        return weight.at[slot // 4 * 2 + slot % 2, rows, pl.ds(slot // 2 % 2 * cols, cols)]
+
     def xcopy(src, slot, peer):
         return pltpu.make_async_remote_copy(
-            src_ref=src, dst_ref=weight.at[slot], send_sem=xsend_sem.at[slot, 0], recv_sem=xrecv_sem.at[slot, 0],
+            src_ref=src, dst_ref=slot_ref(slot), send_sem=xsend_sem.at[slot, 0], recv_sem=xrecv_sem.at[slot, 0],
             device_id=peer, device_id_type=MESH)
 
     def own_parts(half):
@@ -325,12 +342,12 @@
     def own_copies(slot, peer):
         return [
             pltpu.make_async_remote_copy(
-                src_ref=src, dst_ref=weight.at[slot, at], send_sem=xsend_sem.at[slot, j], recv_sem=xrecv_sem.at[slot, j],
+                src_ref=src, dst_ref=slot_ref(slot, into), send_sem=xsend_sem.at[slot, j], recv_sem=xrecv_sem.at[slot, j],
                 device_id=peer, device_id_type=MESH)
-            for j, (src, at) in enumerate(own_parts(slot % 2))
+            for j, (src, into) in enumerate(own_parts(slot % 2)) if j or slot in (2, 3)
         ]
 
-    own_sends = [(4, right), (8, left), (2, sib), (5, right), (9, left), (3, sib)]
+    own_sends = [(4, right), (9, left), (2, sib), (5, right), (8, left), (3, sib)]
     relays = [(6, sib), (7, sib), (10, sib), (11, sib), (12, right), (13, left), (14, sib), (15, sib)]
 
     def x_wait_recv(slot):
@@ -338,16 +355,20 @@
             for copy in own_copies(slot, sib):
                 copy.wait_recv()
         else:
-            xcopy(weight.at[slot], slot, sib).wait_recv()
+            xcopy(slot_ref(slot), slot, sib).wait_recv()
 
     loads = []
     for half in range(2):
         for j, (src, part_rows) in enumerate(own_parts(half)):
-            loads.append(pltpu.make_async_copy(src, weight.at[half, part_rows], load_sem.at[2 * half + j]))
+            loads.append(pltpu.make_async_copy(src, slot_ref(half, part_rows), load_sem.at[2 * half + j]))
+    for side in range(2):
+        for half in range(2):
+            loads.append(pltpu.make_async_copy(
+                pre_hbm.at[side, :, pl.ds(half * cols, cols)], slot_ref(4 + 4 * side + half, pl.ds(0, split)), load_sem.at[4 + 2 * side + half]))
     col = 0
     for idx, act_hbm in enumerate(acts_hbm):
         size = act_hbm.shape[1]
-        loads.append(pltpu.make_async_copy(act_hbm, act.at[:, pl.ds(col, size)], load_sem.at[4 + idx]))
+        loads.append(pltpu.make_async_copy(act_hbm, act.at[:, pl.ds(col, size)], load_sem.at[8 + idx]))
         col += size
     for load in loads:
         load.start()
@@ -432,11 +453,10 @@
 
     def group_info(g):
         mid = jnp.logical_and(g >= 2, g < 6)
-        i = g - 2
-        odd = lax.rem(i + 2, 2)
-        slot = jnp.where(g < 2, g, jnp.where(mid, 4 + 4 * odd + lax.div(i + 2, 2) - 1, g + 6))
-        delta = jnp.where(g < 2, 0, jnp.where(mid, 2 * odd - 1, 2))
-        half = jnp.where(mid, lax.div(i + 2, 2) - 1, lax.rem(g, 2))
+        second, late = lax.rem(g, 2), lax.div(g, 4)
+        half = jnp.where(mid, lax.rem(second + late, 2), second)
+        slot = jnp.where(g < 2, g, jnp.where(mid, 4 + 4 * second + half, g + 6))
+        delta = jnp.where(g < 2, 0, jnp.where(mid, 2 * second - 1, 2))
         chip = lax.rem(lax.div(fs, 2) + delta + 4, 4)
         col_a = pl.multiple_of((chip * 2 + core) * full + half * cols, 128)
         col_b = pl.multiple_of((chip * 2 + 1 - core) * full + half * cols, 128)
@@ -466,27 +486,27 @@
         @pl.when(g == 2)
         def _():
             x_wait_recv(4)
-            xcopy(weight.at[4], 6, sib).start()
-            xcopy(weight.at[4], 12, right).start()
-            x_wait_recv(8)
-            xcopy(weight.at[8], 10, sib).start()
+            xcopy(slot_ref(4), 12, right).start()
+            xcopy(slot_ref(4), 6, sib).start()
+            x_wait_recv(9)
+            xcopy(slot_ref(9), 13, left).start()
+            xcopy(slot_ref(9), 11, sib).start()
 
         @pl.when(g == 4)
         def _():
             x_wait_recv(5)
-            xcopy(weight.at[5], 7, sib).start()
-            x_wait_recv(9)
-            xcopy(weight.at[9], 11, sib).start()
-            xcopy(weight.at[9], 13, left).start()
+            xcopy(slot_ref(5), 7, sib).start()
+            x_wait_recv(8)
+            xcopy(slot_ref(8), 10, sib).start()
 
         @pl.when(g == 6)
         def _():
             x_wait_recv(12)
-            xcopy(weight.at[12], 14, sib).start()
+            xcopy(slot_ref(12), 14, sib).start()
             x_wait_recv(13)
-            xcopy(weight.at[13], 15, sib).start()
-
-        for known, known_slot in enumerate((2, 3, 6, 10, 7, 11, 14, 15)):
+            xcopy(slot_ref(13), 15, sib).start()
+
+        for known, known_slot in enumerate((2, 3, 6, 11, 7, 10, 14, 15)):
             @pl.when(g == known)
             def _():
                 x_wait_recv(known_slot)
@@ -494,9 +514,8 @@
         @pl.loop(0, act.shape[0] // 256)
         def _(m):
             where = pl.ds(pl.multiple_of(m * 256, 256), 256)
-            for j in range(2):
-                value = jnp.dot(act[where, :], weight[slot + 2 * j], preferred_element_type=jnp.float32)
-                part[pslot(g), where, j * cols : (j + 1) * cols] = value.astype(jnp.bfloat16)
+            value = jnp.dot(act[where, :], weight[lax.div(slot, 4) * 2 + lax.rem(slot, 2)], preferred_element_type=jnp.float32)
+            part[pslot(g), where, :] = value.astype(jnp.bfloat16)
 
         for x in range(2):
             start(scatter_far(g, x, 1))
@@ -547,17 +566,17 @@
         relay((gather_near, 1), (gather_far, 1)), stage8,
     ]
 
-    @pl.loop(0, (N_GROUPS // 2 - 1) * PERIOD + 1 + STAGES)
+    @pl.loop(0, (N_GROUPS // 2 - 1) * PERIOD + STAGES)
     def _(t):
         for s in reversed(range(STAGES)):
             d = t - s
-            pair, second = lax.div(d + 2 * PERIOD, PERIOD) - 2, lax.rem(d + 2 * PERIOD, PERIOD)
-            g = 2 * pair + second
-            inside = jnp.logical_and(d >= 0, d < (N_GROUPS // 2) * PERIOD)
-
-            @pl.when(jnp.logical_and(inside, second < 2))
+            pair = lax.div(d + 4 * PERIOD, PERIOD) - 4
+            starts = jnp.logical_and(lax.rem(d + 4 * PERIOD, PERIOD) == 0, jnp.logical_and(d >= 0, d < (N_GROUPS // 2) * PERIOD))
+
+            @pl.when(starts)
             def _():
-                stages[s](g)
+                stages[s](2 * pair)
+                stages[s](2 * pair + 1)
 
     @pl.loop(0, N_GROUPS)
     def _(g):
@@ -567,10 +586,10 @@
         for copy in own_copies(slot, peer):
             copy.wait_send()
     for slot, peer in relays:
-        xcopy(weight.at[slot], slot, peer).wait_send()
-
-
-def second_product(acts, w_out, w_down, rows):
+        xcopy(slot_ref(slot), slot, peer).wait_send()
+
+
+def second_product(acts, pre, w_out, w_down, rows):
     seq_len = rows.shape[0]
     depth = w_out.shape[0] + w_down.shape[0]
     wide = w_out.shape[1]
@@ -578,12 +597,12 @@
     bf16 = jnp.bfloat16
     return pl.pallas_call(
         functools.partial(reduce_kernel, len(acts)),
-        in_specs=[pl.BlockSpec(memory_space=pl.ANY)] * (len(acts) + 3),
+        in_specs=[pl.BlockSpec(memory_space=pl.ANY)] * (len(acts) + 4),
         out_specs=pl.BlockSpec(memory_space=pl.ANY),
         out_shape=jax.ShapeDtypeStruct(rows.shape, bf16),
         scratch_shapes=[
             pltpu.VMEM((seq_len, depth), bf16),
-            pltpu.VMEM((16, depth, cols), bf16),
+            pltpu.VMEM((8, depth, wide), bf16),
             pltpu.VMEM((PART_SLOTS, seq_len, wide), bf16),
             pltpu.VMEM((N_GROUPS, seq_len, wide), bf16),
             pltpu.VMEM((N_GROUPS, 2, 2, ROWS_L1 // 2, wide), bf16),
@@ -595,14 +614,14 @@
             pltpu.SemaphoreType.DMA((N_GROUPS, 2, 16)),
             pltpu.SemaphoreType.DMA((16, 2)),
             pltpu.SemaphoreType.DMA((16, 2)),
-            pltpu.SemaphoreType.DMA((4 + len(acts),)),
+            pltpu.SemaphoreType.DMA((8 + len(acts),)),
             pltpu.SemaphoreType.DMA((N_GROUPS, 4)),
             pltpu.SemaphoreType.DMA((N_GROUPS, 2)),
         ],
         compiler_params=pltpu.CompilerParams(collective_id=0, has_side_effects=True, vmem_limit_bytes=62 * 1024 * 1024),
         cost_estimate=pl.CostEstimate(
             flops=2 * seq_len * depth * rows.shape[1], bytes_accessed=2 * (seq_len * depth + 8 * depth * wide + 2 * rows.size), transcendentals=0),
-    )(*acts, w_out, w_down, rows)
+    )(*acts, pre, w_out, w_down, rows)
 
 
 def solution(mesh):
@@ -611,8 +630,8 @@
     def local_layer(hidden, positions, norm_gain, w_query, w_key, w_value, w_gate, w_up, w_out, w_down):
         rows = hidden[0]
         cos_t, sin_t = rope_tables(positions, w_key.shape[1])
-        acts = first_products(rows, norm_gain, w_query, w_key, w_value, w_gate, w_up, cos_t, sin_t)
-        return second_product(acts, w_out, w_down, rows)[None]
+        *acts, pre = first_products(rows, norm_gain, w_query, w_key, w_value, w_gate, w_up, w_out, cos_t, sin_t)
+        return second_product(acts, pre, w_out, w_down, rows)[None]
 
     in_specs = (row_spec, P(None), P("fsdp"), P("fsdp", "tp"), P("fsdp", None), P("fsdp", None), P("fsdp", "tp"), P("fsdp", "tp"), P("tp", "fsdp"), P("tp", "fsdp"))
     return jax.shard_map(local_layer, mesh=mesh, in_specs=in_specs, out_specs=row_spec, check_vma=False)

time: 416 us -> 392 us (0.942)
  Pallas kernels: 400 us -> 375 us
    pallas_call x1, Pallas kernels: 197 us -> 171 us  [second_product(): pl.pallas_call(functools.partial(reduce_kernel, len(acts)), in_specs=[pl....]
where the time goes in v2:
time: 392 us; the launch traced here: 390 us
  Pallas kernels  375 us (96%)
  local copies, waits for them, and re-layouts  12 us (3%)
    pallas_call x1, Pallas kernels, first_products(): pl.pallas_call(first_kernel, in_specs=[hbm] * 8 + [vmem] * 5, out_specs=[...  204 us
    pallas_call x1, Pallas kernels, second_product(): pl.pallas_call(functools.partial(reduce_kernel, len(acts)), in_specs=[pl....  171 us
    unnamed x1, local copies, waits for them, and re-layouts  10.7 us

profile of v2, /device:TPU:0, one launch (start us, length us, event | category | flops | bytes accessed | tf_op | source)
XLA Modules:
  0.0 390.5 jit_solution(11164917306285382700)
XLA Ops:
  0.0 1.3 reshape.11.gain_hbm
  1.3 0.7 convert_element_type.3
  2.0 0.2 broadcast_multiply_fusion
  2.2 2.9 fusion
  5.1 203.7 %shard_map.127 = (bf16[1024,384]{1,0:T(8,128)(2,1)}, bf16[1024,1536]{1,0:T(8,128)(2,1)}, bf16[2,384,768]{2,1,0:T(8,128)(2,1)}) custom-call(bf16[1024,6144]{1,0:T(8,128)(2,1)} %bitcast.5, f32[1,768]{1,0:T(1,128)} %reshape.11.gain_hbm, bf16[768,384]{1,0:T(8,128)(2,1)} %wq_hbm.1, bf16[96,768]{1,0:T(8,128)(2,1)} %bitcast.7, bf16[96,768]{1,0:T(8,128)(2,1)} %bitcast.8, ...), custom_call_target="tpu_custom_call" | custom-call | tf_op jit(solution)/shard_map/pallas_call | solution.py:265
  208.7 171.0 %shard_map.128 = bf16[1024,6144]{1,0:T(8,128)(2,1)} custom-call(bf16[1024,384]{1,0:T(8,128)(2,1)} %get-tuple-element.8.refs_0_, bf16[1024,1536]{1,0:T(8,128)(2,1)} %get-tuple-element.9.refs_1_, bf16[2,384,768]{2,1,0:T(8,128)(2,1)} %get-tuple-element.10.refs_2_, bf16[384,768]{1,0:T(8,128)(2,1)} %refs_3_.1, bf16[1536,768]{1,0:T(8,128)(2,1)} %refs_4_.1, ...), custom_call_target="tpu_custom_call" | custom-call | flops 24159191040 | bytes 52690944 | tf_op jit(solution)/shard_map/pallas_call | solution.py:598
  379.7 10.7 %copy.15 = bf16[1,1024,6144]{2,1,0:T(8,128)(2,1)} copy(bf16[1,1024,6144]{2,1,0:T(8,128)(2,1)} %bitcast.4) | data formatting | bytes 25165824
  (1 shorter events, 0.0 us)

commit v3 on v2

--- a/solution.py
+++ b/solution.py
@@ -106,14 +106,14 @@
     def gain_copy(slot):
         by_chip, other = places[slot]
         return pltpu.make_async_remote_copy(
-            src_ref=gain_hbm, dst_ref=gains.at[slot], send_sem=gain_send.at[slot], recv_sem=gain_recv.at[slot],
+            src_ref=gain_hbm, dst_ref=gains.at[pl.ds(slot * depth, depth)], send_sem=gain_send.at[slot], recv_sem=gain_recv.at[slot],
             device_id={"fsdp": device(-by_chip, other)}, device_id_type=MESH)
 
     for slot in range(1, n):
         gain_copy(slot).start()
     begin(qkv_streams())
     begin(ff_streams(0))
-    own_gain = pltpu.make_async_copy(gain_hbm, gains.at[0], gain_send.at[0])
+    own_gain = pltpu.make_async_copy(gain_hbm, gains.at[pl.ds(0, depth)], gain_send.at[0])
     own_gain.start()
     blocks = []
     for slot, place in enumerate(places):
@@ -136,7 +136,7 @@
         scaled = centered * lax.rsqrt(variance + NORM_EPS)
         for slot in range(n):
             cols = slice(slot * depth, (slot + 1) * depth)
-            act[where, cols] = (scaled[:, cols] * gains[slot]).astype(jnp.bfloat16)
+            act[where, cols] = (scaled[:, cols] * gains[cols].reshape(1, depth)).astype(jnp.bfloat16)
 
     pass_on(qkv_streams())
     begin(ff_streams(1))
@@ -269,7 +269,7 @@
         out_shape=[jax.ShapeDtypeStruct((seq_len, q_width), bf16), jax.ShapeDtypeStruct((seq_len, ff), bf16), jax.ShapeDtypeStruct((2, *w_out.shape), bf16)],
         scratch_shapes=[
             pltpu.VMEM((seq_len, width), bf16),
-            pltpu.VMEM((8, 1, width // 8), jnp.float32),
+            pltpu.VMEM((width,), jnp.float32),
             pltpu.VMEM((width, q_width), bf16),
             pltpu.VMEM((head_dim, width), bf16),
             pltpu.VMEM((head_dim, width), bf16),
@@ -289,7 +289,7 @@
             pltpu.SemaphoreType.DMA((2,)),
         ],
         compiler_params=pltpu.CompilerParams(collective_id=1, has_side_effects=True, vmem_limit_bytes=67043328),
-    )(rows, norm_gain.reshape(1, -1), w_query, w_key.T, w_value.T, w_gate, w_up, w_out, cos_t, sin_t, pick, pick_rot, place)
+    )(rows, norm_gain, w_query, w_key.T, w_value.T, w_gate, w_up, w_out, cos_t, sin_t, pick, pick_rot, place)
 
 
 ROWS_L1 = 128
@@ -297,6 +297,7 @@
 N_GROUPS = 8
 PERIOD = 3
 STAGES = 9
+SETTLE_PARTS = 16
 PART_SLOTS = 6
 
 
@@ -357,20 +358,26 @@
         else:
             xcopy(slot_ref(slot), slot, sib).wait_recv()
 
-    loads = []
-    for half in range(2):
-        for j, (src, part_rows) in enumerate(own_parts(half)):
-            loads.append(pltpu.make_async_copy(src, slot_ref(half, part_rows), load_sem.at[2 * half + j]))
-    for side in range(2):
-        for half in range(2):
-            loads.append(pltpu.make_async_copy(
-                pre_hbm.at[side, :, pl.ds(half * cols, cols)], slot_ref(4 + 4 * side + half, pl.ds(0, split)), load_sem.at[4 + 2 * side + half]))
+    def own_loads(half):
+        return [
+            pltpu.make_async_copy(src, slot_ref(half, part_rows), load_sem.at[2 * half + j])
+            for j, (src, part_rows) in enumerate(own_parts(half))
+        ]
+
+    def early_loads():
+        return [
+            pltpu.make_async_copy(
+                pre_hbm.at[side, :, pl.ds(half * cols, cols)], slot_ref(4 + 4 * side + half, pl.ds(0, split)), load_sem.at[4 + 2 * side + half])
+            for side in range(2) for half in range(2)
+        ]
+
+    act_loads = []
     col = 0
     for idx, act_hbm in enumerate(acts_hbm):
         size = act_hbm.shape[1]
-        loads.append(pltpu.make_async_copy(act_hbm, act.at[:, pl.ds(col, size)], load_sem.at[8 + idx]))
+        act_loads.append(pltpu.make_async_copy(act_hbm, act.at[:, pl.ds(col, size)], load_sem.at[8 + idx]))
         col += size
-    for load in loads:
+    for load in act_loads + own_loads(0) + own_loads(1) + early_loads():
         load.start()
 
     barrier = pltpu.get_barrier_semaphore()
@@ -382,7 +389,7 @@
     for slot, peer in own_sends:
         for copy in own_copies(slot, peer):
             copy.start()
-    for load in loads:
+    for load in act_loads + own_loads(0):
         load.wait()
 
     halves = [("y", "z"), ("z", "y")]
@@ -483,8 +490,15 @@
         slot, _, _ = group_info(g)
         start(resid_copies(g))
 
+        @pl.when(g == 1)
+        def _():
+            for load in own_loads(1):
+                load.wait()
+
         @pl.when(g == 2)
         def _():
+            for load in early_loads():
+                load.wait()
             x_wait_recv(4)
             xcopy(slot_ref(4), 12, right).start()
             xcopy(slot_ref(4), 6, sib).start()
@@ -511,14 +525,22 @@
             def _():
                 x_wait_recv(known_slot)
 
-        @pl.loop(0, act.shape[0] // 256)
-        def _(m):
-            where = pl.ds(pl.multiple_of(m * 256, 256), 256)
-            value = jnp.dot(act[where, :], weight[lax.div(slot, 4) * 2 + lax.rem(slot, 2)], preferred_element_type=jnp.float32)
-            part[pslot(g), where, :] = value.astype(jnp.bfloat16)
-
+        columns = weight.at[lax.div(slot, 4) * 2 + lax.rem(slot, 2)]
+
+        def product(delta):
+            where = [pl.ds(block1(x, delta), ROWS_L1) for x in range(2)]
+            both = jnp.concatenate([act[rows, :] for rows in where], axis=0)
+            value = jnp.dot(both, columns[...], preferred_element_type=jnp.float32).astype(jnp.bfloat16)
+            for x, rows in enumerate(where):
+                part[pslot(g), rows, :] = value[x * ROWS_L1 : (x + 1) * ROWS_L1]
+
+        product(2)
         for x in range(2):
             start(scatter_far(g, x, 1))
+
+        @pl.loop(0, 3)
+        def _(k):
+            product(k - 1)
 
     def scatter_mid(level):
         def run(g):
@@ -624,6 +646,38 @@
     )(*acts, pre, w_out, w_down, rows)
 
 
+def settle_kernel(src_hbm, out_hbm, buffer, in_sem, out_sem):
+    loads = [pltpu.make_async_copy(src_hbm.at[rows], buffer.at[rows], in_sem.at[k]) for k, rows in enumerate(settle_rows(src_hbm))]
+    stores = [pltpu.make_async_copy(buffer.at[rows], out_hbm.at[rows], out_sem.at[k]) for k, rows in enumerate(settle_rows(src_hbm))]
+    for load in loads:
+        load.start()
+    for load, store in zip(loads, stores):
+        load.wait()
+        store.start()
+    for store in stores:
+        store.wait()
+
+
+def settle_rows(ref):
+    size = ref.shape[0] // SETTLE_PARTS
+    return [pl.ds(k * size, size) for k in range(SETTLE_PARTS)]
+
+
+def settle(result):
+    return pl.pallas_call(
+        settle_kernel,
+        in_specs=[pl.BlockSpec(memory_space=pl.ANY)],
+        out_specs=pl.BlockSpec(memory_space=pl.ANY),
+        out_shape=jax.ShapeDtypeStruct(result.shape, result.dtype),
+        scratch_shapes=[
+            pltpu.VMEM(result.shape, result.dtype),
+            pltpu.SemaphoreType.DMA((SETTLE_PARTS,)),
+            pltpu.SemaphoreType.DMA((SETTLE_PARTS,)),
+        ],
+        compiler_params=pltpu.CompilerParams(vmem_limit_bytes=62 * 1024 * 1024),
+    )(result)
+
+
 def solution(mesh):
     row_spec = P(("dp", "fsdp"), None, None)
 
@@ -631,7 +685,7 @@
         rows = hidden[0]
         cos_t, sin_t = rope_tables(positions, w_key.shape[1])
         *acts, pre = first_products(rows, norm_gain, w_query, w_key, w_value, w_gate, w_up, w_out, cos_t, sin_t)
-        return second_product(acts, pre, w_out, w_down, rows)[None]
+        return settle(second_product(acts, pre, w_out, w_down, rows))[None]
 
     in_specs = (row_spec, P(None), P("fsdp"), P("fsdp", "tp"), P("fsdp", None), P("fsdp", None), P("fsdp", "tp"), P("fsdp", "tp"), P("tp", "fsdp"), P("tp", "fsdp"))
     return jax.shard_map(local_layer, mesh=mesh, in_specs=in_specs, out_specs=row_spec, check_vma=False)

time: 392 us -> 384 us (0.980)
  local copies, waits for them, and re-layouts: 12 us -> 0 us
  Pallas kernels: 375 us -> 380 us
    unnamed x1 -> x0, local copies, waits for them, and re-layouts: 10.7 us -> none
    pallas_call x0 -> x1, Pallas kernels: none -> 9.03 us  [settle(): pl.pallas_call(settle_kernel, in_specs=[pl.BlockSpec(memory_space=pl.ANY)...]
where the time goes in v3:
time: 384 us
  Pallas kernels  380 us (99%)
    pallas_call x1, Pallas kernels, first_products(): pl.pallas_call(first_kernel, in_specs=[hbm] * 8 + [vmem] * 5, out_specs=[...  204 us
    pallas_call x1, Pallas kernels, second_product(): pl.pallas_call(functools.partial(reduce_kernel, len(acts)), in_specs=[pl....  167 us
    pallas_call x1, Pallas kernels, settle(): pl.pallas_call(settle_kernel, in_specs=[pl.BlockSpec(memory_space=pl.ANY)...  9.03 us

profile of v3, /device:TPU:0, one launch (start us, length us, event | category | flops | bytes accessed | tf_op | source)
XLA Modules:
  0.0 384.0 jit_solution(5172064257559324172)
XLA Ops:
  0.0 0.7 convert_element_type.3
  0.7 0.2 broadcast_multiply_fusion
  0.9 2.9 fusion
  3.8 203.7 %shard_map.127 = (bf16[1024,384]{1,0:T(8,128)(2,1)}, bf16[1024,1536]{1,0:T(8,128)(2,1)}, bf16[2,384,768]{2,1,0:T(8,128)(2,1)}) custom-call(bf16[1024,6144]{1,0:T(8,128)(2,1)} %bitcast.4, f32[768]{0:T(1024)} %gain_hbm.1, bf16[768,384]{1,0:T(8,128)(2,1)} %wq_hbm.1, bf16[96,768]{1,0:T(8,128)(2,1)} %bitcast.6, bf16[96,768]{1,0:T(8,128)(2,1)} %bitcast.7, ...), custom_call_target="tpu_custom_call" | custom-call | tf_op jit(solution)/shard_map/pallas_call | solution.py:265
  207.5 167.4 %shard_map.128.src_hbm = bf16[1024,6144]{1,0:T(8,128)(2,1)} custom-call(bf16[1024,384]{1,0:T(8,128)(2,1)} %get-tuple-element.8.refs_0_, bf16[1024,1536]{1,0:T(8,128)(2,1)} %get-tuple-element.9.refs_1_, bf16[2,384,768]{2,1,0:T(8,128)(2,1)} %get-tuple-element.10.refs_2_, bf16[384,768]{1,0:T(8,128)(2,1)} %refs_3_.1, bf16[1536,768]{1,0:T(8,128)(2,1)} %refs_4_.1, ...), custom_call_target="tpu_custom_call" | custom-call | flops 24159191040 | bytes 52690944 | tf_op jit(solution)/shard_map/pallas_call | solution.py:620
  374.8 9.0 %shard_map.129 = bf16[1024,6144]{1,0:T(8,128)(2,1)} custom-call(bf16[1024,6144]{1,0:T(8,128)(2,1)} %shard_map.128.src_hbm), custom_call_target="tpu_custom_call" | custom-call | tf_op jit(solution)/shard_map/pallas_call | solution.py:667
  (1 shorter events, 0.0 us)
